TPU v7x, 128 devices: a whole 4x4x4 slice. The times are simulated.
128 devices in a mesh: dp: 32 (over z, x, core), rep: 4 (over y).
Axes of the slice: x: 4, y: 4, z: 4, core: 2. Of those that a mesh axis runs over, the one named last changes fastest.
Arguments:
- token_inputs: bfloat16 [65536, 2048], P(('dp', 'rep')), may hold values from -12 to 12
- cotangent: bfloat16 [65536, 2048], P(('dp', 'rep')), may hold values from -24 to 24
- gate_preact: bfloat16 [65536, 768], P(('dp', 'rep')), may hold values from -6 to 6
- up_preact: bfloat16 [65536, 768], P(('dp', 'rep')), may hold values from -6 to 6
- down_weight: bfloat16 [2, 768, 2048], P(None, None, 'dp'), may hold values from -0.21875 to 0.21875
- block_expert: int32 [512], P(('dp', 'rep')), may hold values from 0 to 1
- block_count: int32 [512], P(('dp', 'rep')), may hold values from 1 to 128, as said below
Outputs:
- update: bfloat16 [2, 3, 768, 2048], P(None, None, None, 'dp')
Inputs may be any that keep to these rules, and one draw needn't show every extreme that they name: `block_count`: live rows of a block, at most 128; in every draw some block is full.
All inputs are finite; a program needn't handle non-finite values.
Results may differ from a plain program's by a relative error of at most 0.02.
Values may be sent and summed in bfloat16 or wider, within the bound.
No kernel may reach another device: no remote copies, remote signals or barrier semaphores. Data moves between devices by JAX's collectives and lax.ppermute only.
A program may use at most 128 MiB of HBM per device.

v0:
```python
import math
import jax
import jax.numpy as jnp
from jax import lax
from jax.sharding import Mesh
from jax.sharding import PartitionSpec as P

D = 2048
ITERS = 2
DP = ("dp_0", "dp_1", "dp_2")
DP_REP = ("dp_0", "dp_1", "dp_2", "rep")
ns_first = 3.4445
ns_second = -4.775
ns_third = 2.0315
norm_eps = 1e-07


def cut_along(value, dim, count):
    shape = value.shape
    blocks = value.reshape(*shape[:dim], count, shape[dim] // count, *shape[dim + 1 :])
    return jnp.moveaxis(blocks, dim, 0)


def sum_by_chip(value, chips, core, dim):
    sizes = (lax.axis_size(chips), lax.axis_size(core))
    blocks = cut_along(value, dim, sizes[0] * sizes[1])
    inside = blocks.shape[1:]
    blocks = blocks.reshape(*sizes, *inside).swapaxes(0, 1).reshape(-1, *inside)
    blocks = lax.psum_scatter(blocks, core, scatter_dimension=0, tiled=True)
    return lax.psum_scatter(blocks, chips, scatter_dimension=0, tiled=True)[0]


def copy_for_each(value, axis):
    count = lax.axis_size(axis)
    return lax.all_to_all(
        jnp.broadcast_to(value[None], (count, *value.shape)), axis, 0, 0, tiled=True
    )


def of_everyone(value, axis):
    everything = copy_for_each(value, axis)
    return jnp.sum(everything.astype(jnp.float32), axis=0)


def taken_together(value, axis):
    everything = copy_for_each(value, axis)
    return jnp.sum(everything, axis=0)


def whole_sweeps(matrix, column_width, groups_all, sweeps, scale):
    hidden_width = matrix.shape[0]
    group = math.gcd(8, groups_all)
    current = matrix
    result = None
    for sweep in range(sweeps):

        def add_group(index, total):
            cols = lax.dynamic_slice_in_dim(
                current, index * group * column_width, group * column_width, 1
            )
            cols = cols.reshape(hidden_width, group, column_width)
            term = jnp.einsum(
                "fnd,gnd->nfg", cols, cols, preferred_element_type=jnp.float32
            ).astype(jnp.bfloat16)
            return total + jnp.sum(lax.optimization_barrier(term).astype(jnp.float32), axis=0)

        gram = lax.fori_loop(
            0, groups_all // group, add_group, jnp.zeros((hidden_width, hidden_width), jnp.float32)
        )
        gram_half = gram.astype(jnp.bfloat16)
        squared = jnp.dot(gram_half, gram_half, preferred_element_type=jnp.float32)
        poly = (ns_second * gram + ns_third * squared).astype(jnp.bfloat16)
        newer = ns_first * current.astype(jnp.float32) + jnp.dot(
            poly, current, preferred_element_type=jnp.float32
        )
        if sweep + 1 < sweeps:
            current = newer.astype(jnp.bfloat16)
        else:
            result = (scale * newer).astype(jnp.bfloat16)
    return result


def per_device(
    token_inputs, cotangent, gate_preact, up_preact, down_weight, block_expert, block_count
):
    blocks = block_count.shape[0]
    rows_here = token_inputs.shape[0]
    hidden_width = gate_preact.shape[1]
    width = token_inputs.shape[1]
    block_rows = rows_here // blocks
    experts_here = down_weight.shape[0]
    row_place = jnp.arange(rows_here, dtype=jnp.int32) % block_rows
    row_count = jnp.repeat(block_count, block_rows, total_repeat_length=rows_here)
    row_expert = jnp.repeat(block_expert, block_rows, total_repeat_length=rows_here)
    live_rows = row_place < row_count
    masked = jnp.where(live_rows[:, None], cotangent, jnp.zeros_like(cotangent))
    gate = gate_preact.astype(jnp.float32)
    upper = up_preact.astype(jnp.float32)
    sigmoid_gate = jax.nn.sigmoid(gate)
    hidden = (gate * sigmoid_gate * upper).astype(jnp.bfloat16)
    selector = (row_expert[None, :] == jnp.arange(experts_here, dtype=jnp.int32)[:, None]).astype(
        jnp.bfloat16
    )
    masked_each = masked[None, :, :] * selector[:, :, None]
    weights_all = lax.all_gather(down_weight, DP, axis=2, tiled=True)
    back = jnp.einsum("erd,efd->rf", masked_each, weights_all, preferred_element_type=jnp.float32)
    grad_gate = (back * upper * sigmoid_gate * (1.0 + gate * (1.0 - sigmoid_gate))).astype(
        jnp.bfloat16
    )
    grad_up = (back * gate * sigmoid_gate).astype(jnp.bfloat16)
    gate_up = jnp.concatenate([grad_gate, grad_up], axis=1)
    gate_up_each = gate_up[None, :, :] * selector[:, :, None]
    hidden_each = hidden[None, :, :] * selector[:, :, None]
    input_part = jnp.einsum(
        "erf,rd->efd", gate_up_each, token_inputs, preferred_element_type=jnp.float32
    )
    output_part = jnp.einsum("erf,rd->efd", hidden_each, masked, preferred_element_type=jnp.float32)
    partial_value = jnp.concatenate(
        [input_part.reshape(experts_here, 2, hidden_width, width), output_part[:, None]], axis=1
    )
    partial_half = partial_value.astype(jnp.bfloat16)
    terms = lax.optimization_barrier(partial_half).astype(jnp.float32)
    grad = sum_by_chip(terms.astype(jnp.bfloat16), ("dp_0", "dp_1"), "dp_2", 3).astype(jnp.float32)
    grad = of_everyone(grad.astype(jnp.bfloat16), "rep").astype(jnp.float32)
    squares = taken_together(jnp.sum(grad * grad, axis=(2, 3)), DP)
    current = (grad / (jnp.sqrt(squares) + norm_eps)[:, :, None, None]).astype(jnp.bfloat16)
    column_width = current.shape[3]
    scale = jnp.sqrt(jnp.float32(D))
    result = None
    n_dp = lax.axis_size(DP)
    matrices = experts_here * 3
    flat = current.reshape(matrices, hidden_width, column_width)
    padding = jnp.zeros((n_dp - matrices, hidden_width, column_width), jnp.bfloat16)
    outbound = jnp.concatenate([flat, padding], axis=0)
    owned = lax.all_to_all(outbound, DP, split_axis=0, concat_axis=2, tiled=True)
    finished = whole_sweeps(owned[0], column_width, n_dp, ITERS, scale)
    returned = lax.all_to_all(finished[None], DP, split_axis=2, concat_axis=0, tiled=True)
    result = returned[:matrices].reshape(experts_here, 3, hidden_width, column_width)
    return result


def solution(mesh):
    torus = Mesh(mesh.devices.reshape(4, 4, 2, mesh.shape["rep"]), ("dp_0", "dp_1", "dp_2", "rep"))
    return jax.shard_map(
        per_device,
        mesh=torus,
        in_specs=(
            P(DP_REP, None),
            P(DP_REP, None),
            P(DP_REP, None),
            P(DP_REP, None),
            P(None, None, DP),
            P(DP_REP),
            P(DP_REP),
        ),
        out_specs=P(None, None, None, DP),
        check_vma=False,
    )
```

profile of v0, /device:TPU:1, one launch (start us, length us, event | category | flops | bytes accessed | tf_op | source)
XLA Modules:
  0.0 566.8 jit_solution(1773095210929279019)
XLA Ops:
  7.3 1.4 fusion.42
  8.7 2.5 fusion.30
  11.2 1.4 fusion.41
  12.6 2.5 select_select_fusion
  15.2 3.2 broadcast_select_fusion
  18.3 44.0 %all-gather.2.cloned.1.call-done = bf16[2,768,2048]{1,2,0:T(8,128)(2,1)} async-done(((bf16[2,768,64]{1,2,0:T(8,128)(2,1)}), bf16[2,768,2048]{1,2,0:T(8,128)(2,1)}) %all-gather.2.cloned.1.call-update) | async-done | bytes 6291472 | tf_op jit(solution)/shard_map/all_gather | solution.py:105
  62.4 7.8 %fusion.10 = (bf16[512,768]{1,0:T(8,128)(2,1)S(1)}, bf16[512,768]{1,0:T(8,128)(2,1)S(1)}, bf16[512,768]{1,0:T(8,128)(2,1)S(1)}) fusion(bf16[512,768]{1,0:T(8,128)(2,1)} %param.20, bf16[512,768]{1,0:T(8,128)(2,1)} %param.19, bf16[2,768,2048]{1,2,0:T(8,128)(2,1)} %all-gather.2.cloned.1.call-done, bf16[2,512]{1,0:T(2,128)(2,1)S(1)} %compare_convert_fusion, ...), kind=kOutput, calls=%fused_computation.33 | convolution fusion | flops 3230400512 | bytes 12322816 | tf_op jit(solution)/shard_map/erd,efd->rf/dot_general | solution.py:106
  70.2 1.3 pad_maximum_fusion.1
  71.4 2.6 copy.51
  74.0 10.6 %convolution_convert_fusion.2 = bf16[2,1536,2048]{2,1,0:T(8,128)(2,1)} fusion(bf16[512,2048]{1,0:T(8,128)(2,1)S(1)} %copy-done, bf16[2,512]{1,0:T(2,128)(2,1)S(1)} %compare_convert_fusion, bf16[512,1536]{0,1:T(8,128)(2,1)} %copy.51), kind=kOutput, calls=%fused_computation.9 | convolution fusion | flops 6450315264 | bytes 16254976 | tf_op jit(solution)/shard_map/erf,rd->efd/dot_general | solution.py:114
  84.7 16.8 %copy.53 = bf16[2,2,768,2048]{2,3,1,0:T(8,128)(2,1)} copy(bf16[2,2,768,2048]{3,2,1,0:T(8,128)(2,1)} %bitcast.100) | data formatting | bytes 25165824 | tf_op jit(solution)/shard_map/reshape | solution.py:119
  101.4 1.2 copy.52
  102.6 6.3 %convert_bitcast_fusion = bf16[2,1,768,2048]{3,2,0,1:T(8,128)(2,1)} fusion(bf16[512,2048]{1,0:T(8,128)(2,1)S(1)} %copy-done.2, bf16[2,512]{1,0:T(2,128)(2,1)S(1)} %compare_convert_fusion, bf16[512,768]{0,1:T(8,128)(2,1)} %copy.52), kind=kOutput, calls=%fused_computation.12 | convolution fusion | flops 3225157632 | bytes 9177088 | tf_op jit(solution)/shard_map/erf,rd->efd/dot_general | solution.py:117
  108.9 8.7 %copy.54 = bf16[2,1,768,2048]{2,3,1,0:T(8,128)(2,1)} copy(bf16[2,1,768,2048]{3,2,0,1:T(8,128)(2,1)} %convert_bitcast_fusion) | data formatting | bytes 12582912 | tf_op jit(solution)/shard_map/broadcast_in_dim | solution.py:119
  117.6 9.5 %pad_maximum_fusion = bf16[2,3,768,2048]{2,3,1,0:T(8,128)(2,1)S(1)} fusion(bf16[2,1,768,2048]{2,3,1,0:T(8,128)(2,1)} %copy.54, bf16[2,2,768,2048]{2,3,1,0:T(8,128)(2,1)} %copy.53), kind=kLoop, calls=%fused_computation.8 | loop fusion | flops 9437184 | bytes 37748736 | tf_op jit(solution)/shard_map/concatenate | solution.py:118
  127.1 6.7 %copy.55 = bf16[16,2,2,3,768,64]{4,5,3,2,0,1:T(8,128)(2,1)} copy(bf16[16,2,2,3,768,64]{4,5,1,0,3,2:T(8,128)(2,1)S(1)} %bitcast.97) | data formatting | bytes 37748736 | tf_op jit(solution)/shard_map/reshape | solution.py:28
  133.9 28.0 %reduce-scatter.5.cloned.1.call-done = bf16[16,2,3,768,64]{3,4,2,1,0:T(8,128)(2,1)} async-done(((bf16[32,2,3,768,64]{3,4,2,1,0:T(8,128)(2,1)}), bf16[16,2,3,768,64]{3,4,2,1,0:T(8,128)(2,1)}) %reduce-scatter.5.cloned.1.call-update) | async-done | bytes 9437200 | tf_op jit(solution)/shard_map/reduce_scatter | solution.py:29
  161.9 91.3 %reduce-scatter.7.cloned.1.call-done = bf16[1,2,3,768,64]{3,4,2,1,0:T(8,128)(2,1)} async-done(((bf16[16,2,3,768,64]{3,4,2,1,0:T(8,128)(2,1)}), bf16[1,2,3,768,64]{3,4,2,1,0:T(8,128)(2,1)}) %reduce-scatter.7.cloned.1.call-update) | async-done | bytes 589840
  253.2 1.3 broadcast_in_dim.31
  254.5 30.7 %all_to_all.40 = bf16[4,2,3,768,64]{3,4,2,1,0:T(8,128)(2,1)S(1)} all-to-all(bf16[4,2,3,768,64]{3,4,2,1,0:T(8,128)(2,1)S(1)} %broadcast_in_dim.31), channel_id=1, replica_groups=mesh['dp_0'=4,'dp_1'=4,'dp_2'=2,'rep'=4] {'rep'}, dimensions={0} | all-to-all | bytes 4718592 | tf_op jit(solution)/shard_map/all_to_all | solution.py:35
  285.8 15.0 %all_to_all.41 = f32[32,2,3]{2,1,0:T(2,128)S(1)} all-to-all(f32[32,2,3]{2,1,0:T(2,128)S(1)} %broadcast_in_dim.32), channel_id=1, replica_groups=mesh['dp_0'=4,'dp_1'=4,'dp_2'=2,'rep'=4] {'dp_0','dp_1','dp_2'}, dimensions={0} | all-to-all | bytes 1536 | tf_op jit(solution)/shard_map/all_to_all | solution.py:35
  301.3 2.0 concatenate.18
  303.3 5.0 all-to-all-start.2
  308.3 39.9 %all-to-all-done.2 = bf16[32,768,64]{1,2,0:T(8,128)(2,1)} async-done(((bf16[32,768,64]{1,2,0:T(8,128)(2,1)}), bf16[32,768,64]{1,2,0:T(8,128)(2,1)}, u32[]{:S(2)}, u32[]{:S(2)}) %all-to-all-start.2) | async-done | bytes 3145760 | tf_op jit(solution)/shard_map/all_to_all | solution.py:135
  348.2 4.7 copy.58
  352.9 33.6 %while.34 = (s32[]{:T(128)}, f32[768,768]{1,0:T(8,128)}, bf16[768,2048]{0,1:T(8,128)(2,1)}, s32[]{:T(128)}, s32[]{:T(128)}, /*index=5*/s32[]{:T(128)}, s32[]{:T(128)}) while((s32[]{:T(128)}, f32[768,768]{1,0:T(8,128)}, bf16[768,2048]{0,1:T(8,128)(2,1)}, s32[]{:T(128)}, s32[]{:T(128)}, /*index=5*/s32[]{:T(128)}, s32[]{:T(128)}) %tuple.98), condition=%wide.region_7.9_spmd.clone, body=%wide.region_5.8_spmd.clone.sunk | while | flops 618725376 | bytes 30670984 | solution.py:67
  352.9 1.2 constant_dynamic-slice_fusion.4
  354.1 2.9 convolution_convert_fusion.5
  357.0 1.2 convert_reduce_fusion.5
  358.3 1.8 select_add_fusion.4
  360.1 1.2 constant_dynamic-slice_fusion.4
  361.3 2.9 convolution_convert_fusion.5
  364.2 1.2 convert_reduce_fusion.5
  365.4 3.4 select_add_fusion.4
  368.9 1.2 constant_dynamic-slice_fusion.4
  370.1 2.9 convolution_convert_fusion.5
  373.0 1.2 convert_reduce_fusion.5
  374.2 3.4 select_add_fusion.4
  377.7 1.2 constant_dynamic-slice_fusion.4
  378.9 2.9 convolution_convert_fusion.5
  381.8 1.2 convert_reduce_fusion.5
  383.0 3.4 select_add_fusion.4
  386.5 10.5 %add_convert_fusion = bf16[768,2048]{1,0:T(8,128)(2,1)} fusion(bf16[768,2048]{1,0:T(8,128)(2,1)} %copy.58, bf16[768,2048]{0,1:T(8,128)(2,1)} %bitcast.23, f32[768,768]{1,0:T(8,128)} %get-tuple-element.202), kind=kOutput, calls=%fused_computation.11 | convolution fusion | flops 3331129344 | bytes 11796480 | tf_op jit(solution)/shard_map/dot_general | solution.py:73
  397.0 34.4 %while.35 = (s32[]{:T(128)}, f32[768,768]{1,0:T(8,128)}, bf16[768,2048]{1,0:T(8,128)(2,1)}, s32[]{:T(128)}, s32[]{:T(128)}, /*index=5*/s32[]{:T(128)}, s32[]{:T(128)}) while((s32[]{:T(128)}, f32[768,768]{1,0:T(8,128)}, bf16[768,2048]{1,0:T(8,128)(2,1)}, s32[]{:T(128)}, s32[]{:T(128)}, /*index=5*/s32[]{:T(128)}, s32[]{:T(128)}) %tuple.101), condition=%wide.region_10.12_spmd.clone, body=%wide.region_8.11_spmd.clone.sunk | while | flops 618725376 | bytes 32243848 | solution.py:67
  397.0 1.2 constant_dynamic-slice_fusion.5
  398.4 2.9 convolution_convert_fusion.6
  401.3 1.2 convert_reduce_fusion.6
  402.6 1.7 select_add_fusion.5
  405.8 2.9 convolution_convert_fusion.6
  408.7 1.2 convert_reduce_fusion.6
  410.0 3.4 select_add_fusion.5
  414.8 2.9 convolution_convert_fusion.6
  417.7 1.2 convert_reduce_fusion.6
  419.0 3.4 select_add_fusion.5
  423.8 2.9 convolution_convert_fusion.6
  426.7 1.2 convert_reduce_fusion.6
  428.0 3.4 select_add_fusion.5
  431.4 8.5 %fusion.3 = bf16[1,768,2048]{2,1,0:T(8,128)(2,1)S(1)} fusion(bf16[768,2048]{1,0:T(8,128)(2,1)} %get-tuple-element.360, f32[768,768]{1,0:T(8,128)} %get-tuple-element.203), kind=kOutput, calls=%fused_computation.17 | convolution fusion | flops 3332702208 | bytes 8650752 | tf_op jit(solution)/shard_map/dot_general | solution.py:73
  439.9 11.2 %copy.60 = bf16[1,768,2048]{1,0,2:T(2,128)(2,1)} copy(bf16[1,768,2048]{2,1,0:T(8,128)(2,1)S(1)} %fusion.3) | data formatting | bytes 6291456 | tf_op jit(solution)/shard_map/broadcast_in_dim | solution.py:137
  451.7 33.3 %reduce.3 = bf16[2048,768]{1,0:T(8,128)(2,1)} reduce(bf16[2048,1,768]{2,1,0:T(2,128)(2,1)} %bitcast.98, bf16[]{:T(256)} %broadcast.220), dimensions={1}, to_apply=%bitcast.73.reduce_sub_computation | reduce | bytes 6291458
  485.0 6.6 %reshape.174 = bf16[32,2,24576]{2,1,0:T(2,128)(2,1)S(1)} reshape(bf16[2048,768]{1,0:T(8,128)(2,1)} %reduce.3) | data formatting | bytes 6291456
  491.6 45.5 %all_to_all.42 = bf16[32,2,24576]{2,1,0:T(2,128)(2,1)} all-to-all(bf16[32,2,24576]{2,1,0:T(2,128)(2,1)S(1)} %reshape.174), channel_id=1, replica_groups=mesh['dp_0'=4,'dp_1'=4,'dp_2'=2,'rep'=4] {'dp_0','dp_1','dp_2'}, dimensions={0} | all-to-all | bytes 6291456 | tf_op jit(solution)/shard_map/all_to_all | solution.py:137
  537.1 18.9 %reshape.175 = bf16[2048,1,768]{2,1,0:T(2,128)(2,1)} reshape(bf16[32,2,24576]{2,1,0:T(2,128)(2,1)} %all_to_all.42) | data formatting | bytes 6291456
  556.0 3.5 copy.62
  (33 shorter events, 7.9 us)
Async XLA Ops:
  6.5 67.5 %copy-start = (bf16[512,2048]{1,0:T(8,128)(2,1)S(1)}, bf16[512,2048]{1,0:T(8,128)(2,1)}, u32[]{:S(2)}) copy-start(bf16[512,2048]{1,0:T(8,128)(2,1)} %param.17) | copy-start | bytes 6291460
  6.5 55.8 %all-gather.2.cloned.1.call-start = ((), (), s32[]{:S(2)}) async-start(), calls=%async_computation.6 | async-start | bytes 6488064 | tf_op jit(solution)/shard_map/all_gather | solution.py:105
  7.3 154.6 %reduce-scatter.5.cloned.1.call-start = ((), (), s32[]{:S(2)}) async-start(), calls=%async_computation.7 | async-start | bytes 28311552 | tf_op jit(solution)/shard_map/reduce_scatter | solution.py:29
  84.7 18.0 %copy-start.2 = (bf16[512,2048]{1,0:T(8,128)(2,1)S(1)}, bf16[512,2048]{1,0:T(8,128)(2,1)}, u32[]{:S(2)}) copy-start(bf16[512,2048]{1,0:T(8,128)(2,1)} %broadcast_select_fusion) | copy-start | bytes 6291460
  133.8 119.4 %reduce-scatter.7.cloned.1.call-start = ((), (), s32[]{:S(2)}) async-start(), calls=%async_computation.8 | async-start | bytes 10027008
  303.3 44.9 %all-to-all-start.2 = ((bf16[32,768,64]{1,2,0:T(8,128)(2,1)}), bf16[32,768,64]{1,2,0:T(8,128)(2,1)}, u32[]{:S(2)}, u32[]{:S(2)}) async-start(bf16[32,768,64]{1,2,0:T(8,128)(2,1)} %concatenate.18), calls=%async_computation.3 | async-start | bytes 6291456 | tf_op jit(solution)/shard_map/all_to_all | solution.py:135
  556.0 4.3 copy-start.1
Sparse Core Ops, SparseCore 0:
  9.6 52.6 all-gather.1
  133.9 27.9 reduce-scatter.4
  165.4 87.7 reduce-scatter.6
where the time goes:
time: 570 us; the launch traced here: 567 us
  waiting for transfers between devices  204 us (36%)
  local copies, waits for them, and re-layouts  99.3 us (17%)
  blocking collectives  91.1 us (16%)
  other arithmetic  87 us (15%)
  matrix products  66.9 us (12%)
  between operations  13.2 us (2%)
    unnamed x4, waiting for transfers between devices  92 us
    all_to_all x2, blocking collectives, copy_for_each(): lax.all_to_all(jnp.broadcast_to(value[None], (count, *value.shape)), axis...  45.6 us
    all_to_all x1, blocking collectives, per_device(): lax.all_to_all(finished[None], DP, split_axis=2, concat_axis=0, tiled=True)  45.5 us
    all_gather x1, waiting for transfers between devices, per_device(): weights_all = lax.all_gather(down_weight, DP, axis=2, tiled=True)  44 us
    all_to_all x1, waiting for transfers between devices, per_device(): lax.all_to_all(outbound, DP, split_axis=0, concat_axis=2, tiled=True)  39.9 us
    unnamed x3, other arithmetic  33.3 us
    unnamed x11, local copies, waits for them, and re-layouts  29.6 us
    reduce_scatter x1, waiting for transfers between devices, sum_by_chip(): blocks = lax.psum_scatter(blocks, core, scatter_dimension=0, tiled=True)  28 us
  transfers between devices with their start and end apart: 4, of which 4 were waited for; matrix products, arithmetic and copies ran while one was open for 2% of the time, Pallas kernels for 0%

commit v1 on v0

--- a/solution.py
+++ b/solution.py
@@ -134,7 +134,10 @@
     outbound = jnp.concatenate([flat, padding], axis=0)
     owned = lax.all_to_all(outbound, DP, split_axis=0, concat_axis=2, tiled=True)
     finished = whole_sweeps(owned[0], column_width, n_dp, ITERS, scale)
-    returned = lax.all_to_all(finished[None], DP, split_axis=2, concat_axis=0, tiled=True)
+    returned = jnp.concatenate(
+        lax.all_to_all(jnp.stack(jnp.split(finished[None], lax.axis_size(DP), axis=2)), DP, 0, 0),
+        axis=0,
+    )
     result = returned[:matrices].reshape(experts_here, 3, hidden_width, column_width)
     return result
 

time: 570 us -> 527 us (0.925)
  other arithmetic: 87 us -> 53.7 us
  local copies, waits for them, and re-layouts: 99.3 us -> 90.1 us
    unnamed x3 -> x2, other arithmetic: 33.3 us -> 0.01 us
    broadcast_in_dim x1 -> x0, local copies, waits for them, and re-layouts: 11.2 us -> none  [per_device(): finished[None]]
    another operation x0 -> x2, local copies, waits for them, and re-layouts: none -> 7.79 us  [per_device(): jnp.stack(jnp.split(finished[None], lax.axis_size(DP), axis=2))]
    unnamed x11 -> x38, local copies, waits for them, and re-layouts: 29.6 us -> 23.8 us
where the time goes in v1:
time: 527 us; the launch traced here: 525 us
  waiting for transfers between devices  204 us (39%)
  blocking collectives  91.5 us (17%)
  local copies, waits for them, and re-layouts  90.1 us (17%)
  matrix products  66.9 us (13%)
  other arithmetic  53.7 us (10%)
  between operations  13.2 us (3%)
    unnamed x4, waiting for transfers between devices  92 us
    all_to_all x1, blocking collectives, per_device(): lax.all_to_all(jnp.stack(jnp.split(finished[None], lax.axis_size(DP), axi...  45.8 us
    all_to_all x2, blocking collectives, copy_for_each(): lax.all_to_all(jnp.broadcast_to(value[None], (count, *value.shape)), axis...  45.6 us
    all_gather x1, waiting for transfers between devices, per_device(): weights_all = lax.all_gather(down_weight, DP, axis=2, tiled=True)  44 us
    all_to_all x1, waiting for transfers between devices, per_device(): lax.all_to_all(outbound, DP, split_axis=0, concat_axis=2, tiled=True)  39.9 us
    reduce_scatter x1, waiting for transfers between devices, sum_by_chip(): blocks = lax.psum_scatter(blocks, core, scatter_dimension=0, tiled=True)  28 us
    add x8, other arithmetic, add_group(): total + jnp.sum(lax.optimization_barrier(term).astype(jnp.float32), axis=0)  24 us
    unnamed x38, local copies, waits for them, and re-layouts  23.8 us
  transfers between devices with their start and end apart: 4, of which 4 were waited for; matrix products, arithmetic and copies ran while one was open for 2% of the time, Pallas kernels for 0%

profile of v1, /device:TPU:1, one launch (start us, length us, event | category | flops | bytes accessed | tf_op | source)
XLA Modules:
  0.0 524.7 jit_solution(4073043127617027436)
XLA Ops:
  7.3 1.4 fusion.74
  8.7 2.5 fusion.62
  11.2 1.4 fusion.73
  12.6 2.5 select_select_fusion
  15.2 3.2 broadcast_select_fusion
  18.3 44.0 %all-gather.2.cloned.1.call-done = bf16[2,768,2048]{1,2,0:T(8,128)(2,1)} async-done(((bf16[2,768,64]{1,2,0:T(8,128)(2,1)}), bf16[2,768,2048]{1,2,0:T(8,128)(2,1)}) %all-gather.2.cloned.1.call-update) | async-done | bytes 6291472 | tf_op jit(solution)/shard_map/all_gather | solution.py:105
  62.4 7.8 %fusion.10 = (bf16[512,768]{1,0:T(8,128)(2,1)S(1)}, bf16[512,768]{1,0:T(8,128)(2,1)S(1)}, bf16[512,768]{1,0:T(8,128)(2,1)S(1)}) fusion(bf16[512,768]{1,0:T(8,128)(2,1)} %param.20, bf16[512,768]{1,0:T(8,128)(2,1)} %param.19, bf16[2,768,2048]{1,2,0:T(8,128)(2,1)} %all-gather.2.cloned.1.call-done, bf16[2,512]{1,0:T(2,128)(2,1)S(1)} %compare_convert_fusion, ...), kind=kOutput, calls=%fused_computation.33 | convolution fusion | flops 3230400512 | bytes 12322816 | tf_op jit(solution)/shard_map/erd,efd->rf/dot_general | solution.py:106
  70.2 1.3 pad_maximum_fusion.1
  71.4 2.6 copy.51
  74.0 10.6 %convolution_convert_fusion.2 = bf16[2,1536,2048]{2,1,0:T(8,128)(2,1)} fusion(bf16[512,2048]{1,0:T(8,128)(2,1)S(1)} %copy-done, bf16[2,512]{1,0:T(2,128)(2,1)S(1)} %compare_convert_fusion, bf16[512,1536]{0,1:T(8,128)(2,1)} %copy.51), kind=kOutput, calls=%fused_computation.9 | convolution fusion | flops 6450315264 | bytes 16254976 | tf_op jit(solution)/shard_map/erf,rd->efd/dot_general | solution.py:114
  84.7 16.8 %copy.53 = bf16[2,2,768,2048]{2,3,1,0:T(8,128)(2,1)} copy(bf16[2,2,768,2048]{3,2,1,0:T(8,128)(2,1)} %bitcast.221) | data formatting | bytes 25165824 | tf_op jit(solution)/shard_map/reshape | solution.py:119
  101.4 1.2 copy.52
  102.6 6.3 %convert_bitcast_fusion = bf16[2,1,768,2048]{3,2,0,1:T(8,128)(2,1)} fusion(bf16[512,2048]{1,0:T(8,128)(2,1)S(1)} %copy-done.2, bf16[2,512]{1,0:T(2,128)(2,1)S(1)} %compare_convert_fusion, bf16[512,768]{0,1:T(8,128)(2,1)} %copy.52), kind=kOutput, calls=%fused_computation.12 | convolution fusion | flops 3225157632 | bytes 9177088 | tf_op jit(solution)/shard_map/erf,rd->efd/dot_general | solution.py:117
  108.9 8.7 %copy.54 = bf16[2,1,768,2048]{2,3,1,0:T(8,128)(2,1)} copy(bf16[2,1,768,2048]{3,2,0,1:T(8,128)(2,1)} %convert_bitcast_fusion) | data formatting | bytes 12582912 | tf_op jit(solution)/shard_map/broadcast_in_dim | solution.py:119
  117.6 9.5 %pad_maximum_fusion = bf16[2,3,768,2048]{2,3,1,0:T(8,128)(2,1)S(1)} fusion(bf16[2,1,768,2048]{2,3,1,0:T(8,128)(2,1)} %copy.54, bf16[2,2,768,2048]{2,3,1,0:T(8,128)(2,1)} %copy.53), kind=kLoop, calls=%fused_computation.8 | loop fusion | flops 9437184 | bytes 37748736 | tf_op jit(solution)/shard_map/concatenate | solution.py:118
  127.1 6.7 %copy.55 = bf16[16,2,2,3,768,64]{4,5,3,2,0,1:T(8,128)(2,1)} copy(bf16[16,2,2,3,768,64]{4,5,1,0,3,2:T(8,128)(2,1)S(1)} %bitcast.220) | data formatting | bytes 37748736 | tf_op jit(solution)/shard_map/reshape | solution.py:28
  133.9 28.0 %reduce-scatter.5.cloned.1.call-done = bf16[16,2,3,768,64]{3,4,2,1,0:T(8,128)(2,1)} async-done(((bf16[32,2,3,768,64]{3,4,2,1,0:T(8,128)(2,1)}), bf16[16,2,3,768,64]{3,4,2,1,0:T(8,128)(2,1)}) %reduce-scatter.5.cloned.1.call-update) | async-done | bytes 9437200 | tf_op jit(solution)/shard_map/reduce_scatter | solution.py:29
  161.9 91.3 %reduce-scatter.7.cloned.1.call-done = bf16[1,2,3,768,64]{3,4,2,1,0:T(8,128)(2,1)} async-done(((bf16[16,2,3,768,64]{3,4,2,1,0:T(8,128)(2,1)}), bf16[1,2,3,768,64]{3,4,2,1,0:T(8,128)(2,1)}) %reduce-scatter.7.cloned.1.call-update) | async-done | bytes 589840
  253.2 1.3 broadcast_in_dim.31
  254.5 30.7 %all_to_all.30 = bf16[4,2,3,768,64]{3,4,2,1,0:T(8,128)(2,1)S(1)} all-to-all(bf16[4,2,3,768,64]{3,4,2,1,0:T(8,128)(2,1)S(1)} %broadcast_in_dim.31), channel_id=1, replica_groups=mesh['dp_0'=4,'dp_1'=4,'dp_2'=2,'rep'=4] {'rep'}, dimensions={0} | all-to-all | bytes 4718592 | tf_op jit(solution)/shard_map/all_to_all | solution.py:35
  285.8 15.0 %all_to_all.31 = f32[32,2,3]{2,1,0:T(2,128)S(1)} all-to-all(f32[32,2,3]{2,1,0:T(2,128)S(1)} %broadcast_in_dim.32), channel_id=1, replica_groups=mesh['dp_0'=4,'dp_1'=4,'dp_2'=2,'rep'=4] {'dp_0','dp_1','dp_2'}, dimensions={0} | all-to-all | bytes 1536 | tf_op jit(solution)/shard_map/all_to_all | solution.py:35
  301.3 2.0 concatenate.18
  303.3 5.0 all-to-all-start.2
  308.3 39.9 %all-to-all-done.2 = bf16[32,768,64]{1,2,0:T(8,128)(2,1)} async-done(((bf16[32,768,64]{1,2,0:T(8,128)(2,1)}), bf16[32,768,64]{1,2,0:T(8,128)(2,1)}, u32[]{:S(2)}, u32[]{:S(2)}) %all-to-all-start.2) | async-done | bytes 3145760 | tf_op jit(solution)/shard_map/all_to_all | solution.py:135
  348.2 4.7 copy.58
  352.9 33.6 %while.34 = (s32[]{:T(128)}, f32[768,768]{1,0:T(8,128)}, bf16[768,2048]{0,1:T(8,128)(2,1)}, s32[]{:T(128)}, s32[]{:T(128)}, /*index=5*/s32[]{:T(128)}, s32[]{:T(128)}) while((s32[]{:T(128)}, f32[768,768]{1,0:T(8,128)}, bf16[768,2048]{0,1:T(8,128)(2,1)}, s32[]{:T(128)}, s32[]{:T(128)}, /*index=5*/s32[]{:T(128)}, s32[]{:T(128)}) %tuple.98), condition=%wide.region_7.9_spmd.clone, body=%wide.region_5.8_spmd.clone.sunk | while | flops 618725376 | bytes 30670984 | solution.py:67
  352.9 1.2 constant_dynamic-slice_fusion.4
  354.1 2.9 convolution_convert_fusion.5
  357.0 1.2 convert_reduce_fusion.5
  358.3 1.8 select_add_fusion.4
  360.1 1.2 constant_dynamic-slice_fusion.4
  361.3 2.9 convolution_convert_fusion.5
  364.2 1.2 convert_reduce_fusion.5
  365.4 3.4 select_add_fusion.4
  368.9 1.2 constant_dynamic-slice_fusion.4
  370.1 2.9 convolution_convert_fusion.5
  373.0 1.2 convert_reduce_fusion.5
  374.2 3.4 select_add_fusion.4
  377.7 1.2 constant_dynamic-slice_fusion.4
  378.9 2.9 convolution_convert_fusion.5
  381.8 1.2 convert_reduce_fusion.5
  383.0 3.4 select_add_fusion.4
  386.5 10.5 %add_convert_fusion = bf16[768,2048]{1,0:T(8,128)(2,1)} fusion(bf16[768,2048]{1,0:T(8,128)(2,1)} %copy.58, bf16[768,2048]{0,1:T(8,128)(2,1)} %bitcast.23, f32[768,768]{1,0:T(8,128)} %get-tuple-element.202), kind=kOutput, calls=%fused_computation.11 | convolution fusion | flops 3331129344 | bytes 11796480 | tf_op jit(solution)/shard_map/dot_general | solution.py:73
  397.0 34.4 %while.35 = (s32[]{:T(128)}, f32[768,768]{1,0:T(8,128)}, bf16[768,2048]{1,0:T(8,128)(2,1)}, s32[]{:T(128)}, s32[]{:T(128)}, /*index=5*/s32[]{:T(128)}, s32[]{:T(128)}) while((s32[]{:T(128)}, f32[768,768]{1,0:T(8,128)}, bf16[768,2048]{1,0:T(8,128)(2,1)}, s32[]{:T(128)}, s32[]{:T(128)}, /*index=5*/s32[]{:T(128)}, s32[]{:T(128)}) %tuple.101), condition=%wide.region_10.12_spmd.clone, body=%wide.region_8.11_spmd.clone.sunk | while | flops 618725376 | bytes 32243848 | solution.py:67
  397.0 1.2 constant_dynamic-slice_fusion.5
  398.4 2.9 convolution_convert_fusion.6
  401.3 1.2 convert_reduce_fusion.6
  402.6 1.7 select_add_fusion.5
  404.3 1.2 constant_dynamic-slice_fusion.5
  405.8 2.9 convolution_convert_fusion.6
  408.7 1.2 convert_reduce_fusion.6
  410.0 3.4 select_add_fusion.5
  413.3 1.2 constant_dynamic-slice_fusion.5
  414.8 2.9 convolution_convert_fusion.6
  417.7 1.2 convert_reduce_fusion.6
  419.0 3.4 select_add_fusion.5
  422.4 1.2 constant_dynamic-slice_fusion.5
  423.8 2.9 convolution_convert_fusion.6
  426.7 1.2 convert_reduce_fusion.6
  428.0 3.4 select_add_fusion.5
  431.4 8.5 %fusion.3 = bf16[1,768,2048]{2,1,0:T(8,128)(2,1)S(1)} fusion(bf16[768,2048]{1,0:T(8,128)(2,1)} %get-tuple-element.360, f32[768,768]{1,0:T(8,128)} %get-tuple-element.203), kind=kOutput, calls=%fused_computation.17 | convolution fusion | flops 3332702208 | bytes 8650752 | tf_op jit(solution)/shard_map/dot_general | solution.py:73
  464.5 7.0 %copy.60 = bf16[32,1,768,64]{2,3,1,0:T(8,128)(2,1)} copy(bf16[32,1,768,64]{3,2,1,0:T(8,128)(2,1)} %fusion.30) | data formatting | bytes 6291456 | tf_op jit(solution)/shard_map/stack | solution.py:138
  471.5 45.8 %all_to_all.32 = bf16[32,1,768,64]{2,3,1,0:T(8,128)(2,1)S(1)} all-to-all(bf16[32,1,768,64]{2,3,1,0:T(8,128)(2,1)} %copy.60), channel_id=1, replica_groups=mesh['dp_0'=4,'dp_1'=4,'dp_2'=2,'rep'=4] {'dp_0','dp_1','dp_2'}, dimensions={0} | all-to-all | bytes 6291456 | tf_op jit(solution)/shard_map/all_to_all | solution.py:138
  517.3 0.9 slice.46
  (60 shorter events, 27.5 us)
Async XLA Ops:
  6.5 67.5 %copy-start = (bf16[512,2048]{1,0:T(8,128)(2,1)S(1)}, bf16[512,2048]{1,0:T(8,128)(2,1)}, u32[]{:S(2)}) copy-start(bf16[512,2048]{1,0:T(8,128)(2,1)} %param.17) | copy-start | bytes 6291460
  6.5 55.8 %all-gather.2.cloned.1.call-start = ((), (), s32[]{:S(2)}) async-start(), calls=%async_computation.6 | async-start | bytes 6488064 | tf_op jit(solution)/shard_map/all_gather | solution.py:105
  7.3 154.6 %reduce-scatter.5.cloned.1.call-start = ((), (), s32[]{:S(2)}) async-start(), calls=%async_computation.7 | async-start | bytes 28311552 | tf_op jit(solution)/shard_map/reduce_scatter | solution.py:29
  84.7 18.0 %copy-start.2 = (bf16[512,2048]{1,0:T(8,128)(2,1)S(1)}, bf16[512,2048]{1,0:T(8,128)(2,1)}, u32[]{:S(2)}) copy-start(bf16[512,2048]{1,0:T(8,128)(2,1)} %broadcast_select_fusion) | copy-start | bytes 6291460
  133.8 119.4 %reduce-scatter.7.cloned.1.call-start = ((), (), s32[]{:S(2)}) async-start(), calls=%async_computation.8 | async-start | bytes 10027008
  303.3 44.9 %all-to-all-start.2 = ((bf16[32,768,64]{1,2,0:T(8,128)(2,1)}), bf16[32,768,64]{1,2,0:T(8,128)(2,1)}, u32[]{:S(2)}, u32[]{:S(2)}) async-start(bf16[32,768,64]{1,2,0:T(8,128)(2,1)} %concatenate.18), calls=%async_computation.3 | async-start | bytes 6291456 | tf_op jit(solution)/shard_map/all_to_all | solution.py:135
  464.5 53.7 %copy-start.1 = (bf16[512,2048]{1,0:T(8,128)(2,1)S(1)}, bf16[512,2048]{1,0:T(8,128)(2,1)}, u32[]{:S(2)}) copy-start(bf16[512,2048]{1,0:T(8,128)(2,1)} %param.17) | copy-start | bytes 6291460
Sparse Core Ops, SparseCore 0:
  9.6 52.6 all-gather.1
  133.9 27.9 reduce-scatter.4
  165.4 87.7 reduce-scatter.6
